TPU v7x, 32 devices: a whole 2x2x4 slice. The times are simulated.
32 devices in a mesh: dp: 4 (over y, x), seq: 8 (over z, core).
Axes of the slice: x: 2, y: 2, z: 4, core: 2. Of those that a mesh axis runs over, the one named last changes fastest.
Arguments:
- stream: bfloat16 [4, 256, 1536], P('dp', 'seq'), may hold values from -6 to 6
- queries: bfloat16 [4, 256, 1536], P('dp', 'seq'), may hold values from -30 to 30
- new_keys: bfloat16 [4, 256, 1536], P('dp', 'seq'), may hold values from -6.5 to 6.5
- new_values: bfloat16 [4, 256, 1536], P('dp', 'seq'), may hold values from -6 to 6
- cache_keys: bfloat16 [4, 768, 1536], P('dp', 'seq'), may hold values from -6.375 to 6.375
- cache_values: bfloat16 [4, 768, 1536], P('dp', 'seq'), may hold values from -6 to 6
- cache_frames: int32 [4, 768], P('dp', 'seq'), may hold values from 0 to 20, as said below
- group_index: int32 [4], P('dp'), may hold values from 4 to 7, as said below
- timestep: int32 [4], P('dp'), may hold values from 0 to 3
- gate_table: float32 [4, 1536], replicated, may hold values from 0.1 to 1.9
- attn_out_weight: bfloat16 [1536, 1536], replicated, may hold values from -0.15625 to 0.15625
- critic_in: bfloat16 [32768, 1536], P(('dp', 'seq')), may hold values from -6 to 6
- critic_cot: bfloat16 [32768, 1536], P(('dp', 'seq')), may hold values from -6 to 6
- critic_weight: bfloat16 [1536, 1536], P(('dp', 'seq')), may hold values from -0.15625 to 0.15625
Outputs:
- stream_out: bfloat16 [4, 256, 1536], P('dp', 'seq')
- critic_grad_in: bfloat16 [32768, 1536], P(('dp', 'seq'))
- critic_grad_weight: float32 [1536, 1536], P(('dp', 'seq'))
Inputs may be any that keep to these rules, and one draw needn't show every extreme that they name: `group_index`: index of the frame group; both ends are reached in every draw. `cache_frames`: sample b's cache holds the 12 frames 3 * group_index[b] - 12 to 3 * group_index[b] - 1, each in one contiguous run of slots, runs of equal length up to one slot, in a rotated order.
All inputs are finite; a program needn't handle non-finite values.
Results may differ from a plain program's by a relative error of at most 0.0045.
Values may be sent and summed in bfloat16 or wider, within the bound.
A program may use at most 128 MiB of HBM per device.

v0:
```python
import functools

import jax
import jax.numpy as jnp
from jax import lax
from jax.experimental import pallas as pl
from jax.experimental.pallas import tpu as pltpu
from jax.sharding import PartitionSpec as P

HEADS = 12
HEAD = 128
FRAMES_GROUP = 3
WINDOW_FRAMES = 9


def critic_pass(critic_in, critic_cot, critic_weight):
    grad_in = lax.dot_general(
        critic_cot,
        lax.all_gather(critic_weight, ("dp", "seq"), axis=0, tiled=True),
        (((1,), (1,)), ((), ())),
        preferred_element_type=jnp.float32,
    ).astype(jnp.bfloat16)
    factor = float(critic_in.shape[0] * lax.axis_size(("dp", "seq"))) ** (-0.5)
    whole_term = (
        lax.dot_general(
            critic_in, critic_cot, (((0,), (0,)), ((), ())), preferred_element_type=jnp.float32
        )
        * factor
    )
    grad_weight = lax.psum_scatter(whole_term, ("dp", "seq"), scatter_dimension=0, tiled=True)
    return (grad_in, grad_weight)


def by_collectives(
    stream,
    queries,
    new_keys,
    new_values,
    cache_keys,
    cache_values,
    cache_frames,
    group_index,
    timestep,
    gate_table,
    attn_out_weight,
    critic_in,
    critic_cot,
    critic_weight,
):
    query_local = queries[0]
    own_rows = query_local.shape[0]
    width = query_local.shape[1]
    scale = HEAD ** (-0.5)
    first_frame = FRAMES_GROUP * group_index[0]
    frames = cache_frames[0]
    live_cache = (frames < first_frame) & (frames >= first_frame - WINDOW_FRAMES)
    live_local = jnp.concatenate([live_cache, jnp.ones((own_rows,), dtype=bool)])
    keys_local = jnp.concatenate([cache_keys[0], new_keys[0]], axis=0)
    values_local = jnp.concatenate([cache_values[0], new_values[0]], axis=0)
    all_queries = lax.all_gather(queries, "seq", axis=1, tiled=True)[0]
    total_rows = all_queries.shape[0]
    query_heads = all_queries.reshape(total_rows, HEADS, HEAD)
    key_heads = keys_local.reshape(-1, HEADS, HEAD)
    value_heads = values_local.reshape(-1, HEADS, HEAD)
    scores = (
        jnp.einsum("qhd,khd->hqk", query_heads, key_heads, preferred_element_type=jnp.float32)
        * scale
    )
    scores = jnp.where(live_local[None, None, :], scores, -1e30)
    local_top = jnp.max(scores, axis=2)
    global_top = lax.pmax(local_top, "seq")
    weights = jnp.where(live_local[None, None, :], jnp.exp(scores - global_top[:, :, None]), 0.0)
    totals = jnp.sum(weights, axis=2)
    summed = jnp.einsum(
        "hqk,khd->qhd",
        weights.astype(jnp.bfloat16),
        value_heads,
        preferred_element_type=jnp.float32,
    )
    own_sums, own_totals = (
        lax.psum_scatter(summed.reshape(total_rows, width), "seq", scatter_dimension=0, tiled=True),
        lax.psum_scatter(totals.T, "seq", scatter_dimension=0, tiled=True),
    )
    mixed = (
        (own_sums.reshape(own_rows, HEADS, HEAD) / own_totals[:, :, None])
        .reshape(own_rows, width)
        .astype(jnp.bfloat16)
    )
    projected = jnp.dot(mixed, attn_out_weight, preferred_element_type=jnp.float32)
    onehot = (
        timestep[:, None] == jnp.arange(gate_table.shape[0], dtype=jnp.int32)[None, :]
    ).astype(jnp.float32)
    gate = jnp.dot(onehot, gate_table, precision=lax.Precision.HIGHEST)
    stream_out = (stream[0].astype(jnp.float32) + gate * projected).astype(jnp.bfloat16)[None]
    grad_in, grad_weight = critic_pass(critic_in, critic_cot, critic_weight)
    return (stream_out, grad_in, grad_weight)


def step_kernel(
    zs,
    parts,
    stream,
    queries,
    new_keys,
    new_values,
    cache_keys,
    cache_values,
    frames,
    group_index,
    timestep,
    gate_table,
    out_weight_hbm,
    critic_in_hbm,
    critic_cot_hbm,
    weight_shard,
    stream_out,
    grad_in_hbm,
    grad_weight,
    diag_rows,
    cin,
    cot,
    out_weight,
    wfull,
    gmine,
    psend,
    precv,
    dsend,
    xsend,
    ysend,
    rx_diag,
    ry_diag,
    rx_block,
    ry_block,
    osum,
    zsend,
    zrecv,
    gin,
    q_all,
    kfull,
    vfull,
    frames_recv,
    live_row,
    asend,
    arecv,
    ssend,
    srecv,
    mixed,
    send_sems,
    recv_sems,
    local_sems,
):
    f32, bf16 = jnp.float32, jnp.bfloat16
    dp, seq = lax.axis_index("dp"), lax.axis_index("seq")
    z, core = seq // 2, lax.rem(seq, 2)
    other = 1 - core
    tokens, width = cin.shape
    block = width // 4
    shard = block // (2 * zs)
    half = width // 2
    own_q = queries.shape[0]
    cached, fresh = cache_keys.shape[0], new_keys.shape[0]
    keys_one = cached + fresh
    heads_here = half // HEAD
    zh = zs // 2
    dp_x = dp + 1 - 2 * lax.rem(dp, 2)
    dp_y = lax.rem(dp + 2, 4)
    dp_d = dp_x + 2 - 4 * (dp_x // 2)
    order = (dp_d, dp_x, dp_y, dp)
    xn, yn, pair = (dp_x, seq), (dp_y, seq), (dp, z * 2 + other)

    loads = [
        pltpu.make_async_copy(critic_in_hbm, cin, local_sems.at[0]),
        pltpu.make_async_copy(critic_cot_hbm, cot, local_sems.at[1]),
        pltpu.make_async_copy(out_weight_hbm, out_weight, local_sems.at[2]),
    ]
    for load in loads:
        load.start()

    group = []
    for j in range(zs):
        for cc in range(2):
            if j or cc:
                zt = lax.rem(z + j, zs)
                ct = core if cc == 0 else other
                group.append((j, cc, zt, ct))
    barrier = pltpu.get_barrier_semaphore()
    peers = [xn, yn] + [(dp, zt * 2 + ct) for (_, _, zt, ct) in group]
    for peer in peers:
        pl.semaphore_signal(
            barrier, inc=1, device_id=peer, device_id_type=pl.DeviceIdType.MESH
        )
    pl.semaphore_wait(barrier, len(peers))

    sent = []

    def send(src, dst, peer):
        n = len(sent)
        copy = pltpu.make_async_remote_copy(
            src_ref=src,
            dst_ref=dst,
            send_sem=send_sems.at[n],
            recv_sem=recv_sems.at[n],
            device_id=peer,
            device_id_type=pl.DeviceIdType.MESH,
        )
        copy.start()
        sent.append(copy)
        return copy

    other_cols = pl.ds(pl.multiple_of(other * half, 128), half)
    own_cols = pl.ds(pl.multiple_of(core * half, 128), half)

    early = []
    for j, cc, zt, ct in group:
        cols = own_cols if cc == 0 else other_cols
        early.append(send(queries.at[:, cols], q_all.at[seq], (dp, zt * 2 + ct)))
    w_z, w_x, w_y, w_p = [], [], [], []
    for j in range(1, zs):
        zt = lax.rem(z + j, zs)
        w_z.append(send(weight_shard, wfull.at[dp, z, core], (dp, zt * 2 + core)))
    for into, peer in ((w_x, xn), (w_y, yn), (w_p, pair)):
        into.append(send(weight_shard, wfull.at[dp, z, core], peer))
    early.append(
        send(cache_keys.at[:, other_cols], kfull.at[pl.ds(keys_one, cached)], pair)
    )
    early.append(
        send(new_keys.at[:, other_cols], kfull.at[pl.ds(keys_one + cached, fresh)], pair)
    )
    early.append(
        send(cache_values.at[:, other_cols], vfull.at[pl.ds(keys_one, cached)], pair)
    )
    early.append(
        send(new_values.at[:, other_cols], vfull.at[pl.ds(keys_one + cached, fresh)], pair)
    )
    early.append(send(frames, frames_recv, pair))

    wfull[dp, z, core] = weight_shard[...]
    q_all[seq] = queries[:, own_cols]
    kfull[0:cached] = cache_keys[:, own_cols]
    kfull[cached:keys_one] = new_keys[:, own_cols]
    vfull[0:cached] = cache_values[:, own_cols]
    vfull[cached:keys_one] = new_values[:, own_cols]

    loads[0].wait()
    loads[1].wait()
    tile = 512 if width % 512 == 0 else 128

    def grad_block(b):
        rows = pl.ds(pl.multiple_of(order[b] * block, 128), block)

        def body(t, carry):
            cols = pl.ds(pl.multiple_of(t * tile, tile), tile)
            acc = lax.dot_general(
                cin[:, rows],
                cot[:, cols],
                (((0,), (0,)), ((), ())),
                preferred_element_type=f32,
            )
            for k in range(zs):
                lo = acc[2 * k * shard : (2 * k + 1) * shard]
                hi = acc[(2 * k + 1) * shard : (2 * k + 2) * shard]
                gmine[b, k, :, cols] = jnp.where(core == 0, lo, hi)
                psend[b, k, :, cols] = jnp.where(core == 0, hi, lo).astype(bf16)
            return carry

        lax.fori_loop(0, width // tile, body, 0)
        return send(psend.at[b], precv.at[b], pair)

    def chip_sum(b, k):
        return gmine[b, k] + precv[b, k].astype(f32)

    pair_d = grad_block(0)
    pair_x = grad_block(1)
    pair_d.wait_recv()
    for k in range(zs):
        dsend[k] = chip_sum(0, k).astype(bf16)
    diag_x = send(dsend.at[pl.ds(0, zh)], rx_diag, xn)
    diag_y = send(dsend.at[pl.ds(zh, zs - zh)], ry_diag, yn)
    pair_y = grad_block(2)
    pair_x.wait_recv()
    for k in range(zh):
        xsend[k] = chip_sum(1, k).astype(bf16)
    x_first = send(xsend.at[pl.ds(0, zh)], rx_block.at[pl.ds(0, zh)], xn)
    pair_y.wait_recv()
    for k in range(zh, zs):
        ysend[k] = chip_sum(2, k).astype(bf16)
    y_second = send(ysend.at[pl.ds(zh, zs - zh)], ry_block.at[pl.ds(zh, zs - zh)], yn)
    pair_o = grad_block(3)
    diag_x.wait_recv()
    for k in range(zh):
        ysend[k] = (chip_sum(2, k) + rx_diag[k].astype(f32)).astype(bf16)
    y_first = send(ysend.at[pl.ds(0, zh)], ry_block.at[pl.ds(0, zh)], yn)
    diag_y.wait_recv()
    for k in range(zh, zs):
        xsend[k] = (chip_sum(1, k) + ry_diag[k - zh].astype(f32)).astype(bf16)
    x_second = send(xsend.at[pl.ds(zh, zs - zh)], rx_block.at[pl.ds(zh, zs - zh)], xn)

    for j in range(1, zs):
        w_z[j - 1].wait_recv()
        held = wfull.at[dp, lax.rem(z + zs - j, zs), core]
        for into, peer in ((w_x, xn), (w_y, yn), (w_p, pair)):
            into.append(send(held, held, peer))

    for copy in early:
        copy.wait_recv()
    first_frame = FRAMES_GROUP * group_index[0]
    live_row[...] = jnp.ones_like(live_row)
    for at, held in ((0, frames), (keys_one, frames_recv)):
        f = held[...]
        ok = (f < first_frame) & (f >= first_frame - WINDOW_FRAMES)
        live_row[:, at : at + cached] = jnp.where(ok, 1.0, 0.0)
    live = live_row[...] > 0.5
    rows_q = 2 * zs * own_q
    lane = lax.broadcasted_iota(jnp.int32, (rows_q, 128), 1)
    stats = jnp.zeros((rows_q, 128), f32)
    for h in range(heads_here):
        cols = slice(h * HEAD, (h + 1) * HEAD)
        q_head = q_all[:, :, cols].reshape(rows_q, HEAD)
        scores = lax.dot_general(
            q_head, kfull[:, cols], (((1,), (1,)), ((), ())), preferred_element_type=f32
        ) * (HEAD ** (-0.5))
        scores = jnp.where(live, scores, -1e30)
        top = jnp.max(scores, axis=1, keepdims=True)
        weights = jnp.where(live, jnp.exp(scores - top), 0.0)
        total = jnp.sum(weights, axis=1, keepdims=True)
        summed = jnp.dot(weights.astype(bf16), vfull[:, cols], preferred_element_type=f32)
        asend[:, :, cols] = summed.astype(bf16).reshape(2 * zs, own_q, HEAD)
        stats = jnp.where(lane == h, top, stats)
        stats = jnp.where(lane == 64 + h, total, stats)
    ssend[...] = stats.reshape(2 * zs, own_q, 128)
    late = []
    for j, cc, zt, ct in group:
        peer = (dp, zt * 2 + ct)
        late.append(send(asend.at[zt * 2 + ct], arecv.at[j * 2 + cc], peer))
        late.append(send(ssend.at[zt * 2 + ct], srecv.at[j * 2 + cc], peer))
    arecv[0] = asend[seq]
    srecv[0] = ssend[seq]

    w_px, w_py, w_diag = [], [], []

    def pass_on(j):
        zf = lax.rem(z + zs - j, zs)
        w_x[j].wait_recv()
        held = wfull.at[dp_x, zf, core]
        if j < zh:
            w_diag.append(send(held, held, yn))
        w_px.append(send(held, held, pair))
        w_y[j].wait_recv()
        held = wfull.at[dp_y, zf, core]
        if j >= zh:
            w_diag.append(send(held, held, xn))
        w_py.append(send(held, held, pair))

    stores = []

    def grad_in_block(b):
        rows = wfull[order[b]].reshape(block, width)
        step = 256

        def body(t, carry):
            at = pl.ds(pl.multiple_of(t * step, step), step)
            gin[b, at] = lax.dot_general(
                cot[at], rows, (((1,), (1,)), ((), ())), preferred_element_type=f32
            ).astype(bf16)
            return carry

        lax.fori_loop(0, tokens // step, body, 0)
        store = pltpu.make_async_copy(
            gin.at[b],
            grad_in_hbm.at[:, pl.ds(pl.multiple_of(order[b] * block, 128), block)],
            local_sems.at[3 + b],
        )
        store.start()
        stores.append(store)

    pass_on(0)
    for copy in w_p:
        copy.wait_recv()
    grad_in_block(3)

    pair_o.wait_recv()
    x_first.wait_recv()
    x_second.wait_recv()
    y_first.wait_recv()
    y_second.wait_recv()
    for k in range(zs):
        osum[k] = chip_sum(3, k) + rx_block[k].astype(f32) + ry_block[k].astype(f32)
    z_parts = []
    for j in range(1, zs):
        zt = lax.rem(z + j, zs)
        zsend[j - 1] = osum[zt].astype(bf16)
        z_parts.append(send(zsend.at[j - 1], zrecv.at[j - 1], (dp, zt * 2 + core)))

    for j in range(1, zs):
        pass_on(j)

    for copy in late:
        copy.wait_recv()
    for cc in range(2):
        ct = core if cc == 0 else other
        for h in range(heads_here):
            cols = slice(h * HEAD, (h + 1) * HEAD)
            tops = [srecv[j * 2 + cc][:, h : h + 1] for j in range(zs)]
            sums = [srecv[j * 2 + cc][:, 64 + h : 65 + h] for j in range(zs)]
            top = functools.reduce(jnp.maximum, tops)
            acc = jnp.zeros((own_q, HEAD), f32)
            total = jnp.zeros((own_q, 1), f32)
            for j in range(zs):
                scale = jnp.exp(tops[j] - top)
                acc = acc + scale * arecv[j * 2 + cc][:, cols].astype(f32)
                total = total + scale * sums[j]
            at = pl.ds(pl.multiple_of(ct * half + h * HEAD, 128), HEAD)
            mixed[:, at] = (acc / total).astype(bf16)
    loads[2].wait()
    gate = jnp.zeros((1, width), f32)
    for s in range(gate_table.shape[0]):
        gate = gate + jnp.where(timestep[0] == s, gate_table[s : s + 1], 0.0)
    projected = jnp.dot(mixed[...], out_weight[...], preferred_element_type=f32)
    stream_out[...] = (stream[...].astype(f32) + gate * projected).astype(bf16)

    for copy in w_px:
        copy.wait_recv()
    grad_in_block(1)
    for copy in w_py:
        copy.wait_recv()
    grad_in_block(2)
    w_pd = []
    for j in range(zs):
        w_diag[j].wait_recv()
        held = wfull.at[dp_d, lax.rem(z + zs - j, zs), core]
        w_pd.append(send(held, held, pair))

    factor = float(tokens * parts) ** (-0.5)
    for copy in z_parts:
        copy.wait_recv()
    grad = osum[z]
    for j in range(1, zs):
        grad = grad + zrecv[j - 1].astype(f32)
    grad_weight[...] = grad * factor

    for copy in w_pd:
        copy.wait_recv()
    keep = pltpu.make_async_copy(wfull.at[dp_d], diag_rows, local_sems.at[3])
    keep.start()
    stores.append(keep)

    for copy in sent:
        copy.wait_send()
    for store in stores:
        store.wait()


def finish_kernel(stream_part, weight_part, grad_part, cot, diag_rows, stream_out, grad_weight, grad_in):
    stream_out[...] = stream_part[...]
    grad_weight[...] = weight_part[...]
    grad_in[...] = grad_part[...]
    width = cot.shape[1]
    block = width // 4
    dp = lax.axis_index("dp")
    dp_x = dp + 1 - 2 * lax.rem(dp, 2)
    dp_d = dp_x + 2 - 4 * (dp_x // 2)
    rows = diag_rows[...].reshape(block, width)
    grad_in[:, pl.ds(pl.multiple_of(dp_d * block, 128), block)] = lax.dot_general(
        cot[...], rows, (((1,), (1,)), ((), ())), preferred_element_type=jnp.float32
    ).astype(grad_in.dtype)


def fused(
    stream,
    queries,
    new_keys,
    new_values,
    cache_keys,
    cache_values,
    cache_frames,
    group_index,
    timestep,
    gate_table,
    attn_out_weight,
    critic_in,
    critic_cot,
    critic_weight,
):
    bf16, f32 = jnp.bfloat16, jnp.float32
    zs = lax.axis_size("seq") // 2
    parts = lax.axis_size(("dp", "seq"))
    tokens, width = critic_in.shape
    own_q = queries.shape[1]
    shard = critic_weight.shape[0]
    cached, fresh = cache_keys.shape[1], new_keys.shape[1]
    half = width // 2
    keys_two = 2 * (cached + fresh)
    zh = zs // 2
    messages = (2 * zs - 1) * 3 + 5 + (zs - 1) * 2 + 10 + 7 * zs
    vm = pl.BlockSpec(memory_space=pltpu.VMEM)
    sm = pl.BlockSpec(memory_space=pltpu.SMEM)
    hbm = pl.BlockSpec(memory_space=pl.ANY)
    stream_part, grad_part, weight_part, diag_rows = pl.pallas_call(
        functools.partial(step_kernel, zs, parts),
        out_shape=(
            jax.ShapeDtypeStruct(stream.shape[1:], bf16),
            jax.ShapeDtypeStruct((tokens, width), bf16),
            jax.ShapeDtypeStruct((shard, width), f32),
            jax.ShapeDtypeStruct((zs, 2, shard, width), bf16),
        ),
        in_specs=[vm] * 7 + [sm] * 2 + [vm] + [hbm] * 3 + [vm],
        out_specs=(vm, hbm, vm, hbm),
        scratch_shapes=[
            pltpu.VMEM((tokens, width), bf16),
            pltpu.VMEM((tokens, width), bf16),
            pltpu.VMEM((width, width), bf16),
            pltpu.VMEM((4, zs, 2, shard, width), bf16),
            pltpu.VMEM((4, zs, shard, width), f32),
            pltpu.VMEM((4, zs, shard, width), bf16),
            pltpu.VMEM((4, zs, shard, width), bf16),
            pltpu.VMEM((zs, shard, width), bf16),
            pltpu.VMEM((zs, shard, width), bf16),
            pltpu.VMEM((zs, shard, width), bf16),
            pltpu.VMEM((zh, shard, width), bf16),
            pltpu.VMEM((zs - zh, shard, width), bf16),
            pltpu.VMEM((zs, shard, width), bf16),
            pltpu.VMEM((zs, shard, width), bf16),
            pltpu.VMEM((zs, shard, width), f32),
            pltpu.VMEM((zs - 1, shard, width), bf16),
            pltpu.VMEM((zs - 1, shard, width), bf16),
            pltpu.VMEM((4, tokens, width // 4), bf16),
            pltpu.VMEM((2 * zs, own_q, half), bf16),
            pltpu.VMEM((keys_two, half), bf16),
            pltpu.VMEM((keys_two, half), bf16),
            pltpu.VMEM((1, cached), jnp.int32),
            pltpu.VMEM((1, keys_two), f32),
            pltpu.VMEM((2 * zs, own_q, half), bf16),
            pltpu.VMEM((2 * zs, own_q, half), bf16),
            pltpu.VMEM((2 * zs, own_q, 128), f32),
            pltpu.VMEM((2 * zs, own_q, 128), f32),
            pltpu.VMEM((own_q, width), bf16),
            pltpu.SemaphoreType.DMA((messages,)),
            pltpu.SemaphoreType.DMA((messages,)),
            pltpu.SemaphoreType.DMA((7,)),
        ],
        compiler_params=pltpu.CompilerParams(
            collective_id=0, has_side_effects=True, vmem_limit_bytes=60 * 1024 * 1024
        ),
    )(
        stream[0],
        queries[0],
        new_keys[0],
        new_values[0],
        cache_keys[0],
        cache_values[0],
        cache_frames,
        group_index,
        timestep,
        gate_table,
        attn_out_weight,
        critic_in,
        critic_cot,
        critic_weight,
    )
    rows = 256

    def whole(shape):
        return pl.BlockSpec(shape, lambda i: (0,) * len(shape))

    tiles = pl.BlockSpec((rows, width), lambda i: (i, 0))
    small = [whole((own_q, width)), whole((shard, width))]
    stream_out, grad_weight, grad_in = pl.pallas_call(
        finish_kernel,
        grid=(tokens // rows,),
        out_shape=(
            jax.ShapeDtypeStruct((own_q, width), bf16),
            jax.ShapeDtypeStruct((shard, width), f32),
            jax.ShapeDtypeStruct((tokens, width), bf16),
        ),
        in_specs=small + [tiles, tiles, whole((zs, 2, shard, width))],
        out_specs=tuple(small + [tiles]),
    )(stream_part, weight_part, grad_part, critic_cot, diag_rows)
    return (stream_out[None], grad_in, grad_weight)


def local(*args):
    shard, tokens = args[13].shape[0], args[11].shape[0]
    fits = (
        lax.axis_size("dp") == 4
        and lax.axis_size("seq") % 4 == 0
        and shard % 16 == 0
        and args[1].shape[1] % 16 == 0
        and args[4].shape[1] % 16 == 0
        and args[1].shape[2] % 512 == 0
        and tokens % 256 == 0
    )
    return fused(*args) if fits else by_collectives(*args)


def solution(mesh):
    return jax.shard_map(
        local,
        mesh=mesh,
        in_specs=(
            P("dp", "seq", None),
            P("dp", "seq", None),
            P("dp", "seq", None),
            P("dp", "seq", None),
            P("dp", "seq", None),
            P("dp", "seq", None),
            P("dp", "seq"),
            P("dp"),
            P("dp"),
            P(),
            P(),
            P(("dp", "seq"), None),
            P(("dp", "seq"), None),
            P(("dp", "seq"), None),
        ),
        out_specs=(P("dp", "seq", None), P(("dp", "seq"), None), P(("dp", "seq"), None)),
        check_vma=False,
    )
```

profile of v0, /device:TPU:31, one launch (start us, length us, event | category | flops | bytes accessed | tf_op | source)
XLA Modules:
  0.0 66.5 jit_solution(4859075833143629643)
XLA Ops:
  1.9 58.1 %shard_map.157 = (bf16[32,1536]{1,0:T(8,128)(2,1)}, bf16[1024,1536]{1,0:T(8,128)(2,1)}, f32[48,1536]{1,0:T(8,128)}, bf16[4,2,48,1536]{3,2,1,0:T(8,128)(2,1)}) custom-call(bf16[32,1536]{1,0:T(8,128)(2,1)} %bitcast.9, bf16[32,1536]{1,0:T(8,128)(2,1)} %bitcast.10, bf16[32,1536]{1,0:T(8,128)(2,1)} %bitcast.11, bf16[32,1536]{1,0:T(8,128)(2,1)} %bitcast.12, ...), custom_call_target="tpu_custom_call" | custom-call | tf_op jit(solution)/shard_map/pallas_call | solution.py:498
  60.0 6.6 %shard_map.158 = (bf16[32,1536]{1,0:T(8,128)(2,1)}, f32[48,1536]{1,0:T(8,128)}, bf16[1024,1536]{1,0:T(8,128)(2,1)}) custom-call(bf16[32,1536]{1,0:T(8,128)(2,1)} %get-tuple-element.10.stream_part, f32[48,1536]{1,0:T(8,128)} %get-tuple-element.11.weight_part, bf16[1024,1536]{1,0:T(8,128)(2,1)} %get-tuple-element.12.grad_part, bf16[1024,1536]{1,0:T(8,128)(2,1)} %cot.1, ...), custom_call_target="tpu_custom_call" | custom-call | tf_op jit(solution)/shard_map/pallas_call | solution.py:567
where the time goes:
time: 66.7 us; the launch traced here: 66.5 us
  Pallas kernels  64.6 us (97%)
  between operations  1.93 us (3%)
    pallas_call x1, Pallas kernels, fused(): pl.pallas_call(functools.partial(step_kernel, zs, parts), out_shape=(jax....  58.1 us
    pallas_call x1, Pallas kernels, fused(): pl.pallas_call(finish_kernel, grid=(tokens // rows,), out_shape=(jax.Shap...  6.55 us

commit v1 on v0

v1 whole, which is shorter than its diff:
```python
import functools

import jax
import jax.numpy as jnp
from jax import lax
from jax.experimental import pallas as pl
from jax.experimental.pallas import tpu as pltpu
from jax.sharding import PartitionSpec as P

HEADS = 12
HEAD = 128
FRAMES_GROUP = 3
WINDOW_FRAMES = 9
VMEM_LIMIT = 44 * 1024 * 1024
FINISH_LIMIT = 8 * 1024 * 1024


def critic_pass(critic_in, critic_cot, critic_weight):
    grad_in = lax.dot_general(
        critic_cot,
        lax.all_gather(critic_weight, ("dp", "seq"), axis=0, tiled=True),
        (((1,), (1,)), ((), ())),
        preferred_element_type=jnp.float32,
    ).astype(jnp.bfloat16)
    factor = float(critic_in.shape[0] * lax.axis_size(("dp", "seq"))) ** (-0.5)
    whole_term = (
        lax.dot_general(
            critic_in, critic_cot, (((0,), (0,)), ((), ())), preferred_element_type=jnp.float32
        )
        * factor
    )
    grad_weight = lax.psum_scatter(whole_term, ("dp", "seq"), scatter_dimension=0, tiled=True)
    return (grad_in, grad_weight)


def by_collectives(
    stream,
    queries,
    new_keys,
    new_values,
    cache_keys,
    cache_values,
    cache_frames,
    group_index,
    timestep,
    gate_table,
    attn_out_weight,
    critic_in,
    critic_cot,
    critic_weight,
):
    query_local = queries[0]
    own_rows = query_local.shape[0]
    width = query_local.shape[1]
    scale = HEAD ** (-0.5)
    first_frame = FRAMES_GROUP * group_index[0]
    frames = cache_frames[0]
    live_cache = (frames < first_frame) & (frames >= first_frame - WINDOW_FRAMES)
    live_local = jnp.concatenate([live_cache, jnp.ones((own_rows,), dtype=bool)])
    keys_local = jnp.concatenate([cache_keys[0], new_keys[0]], axis=0)
    values_local = jnp.concatenate([cache_values[0], new_values[0]], axis=0)
    all_queries = lax.all_gather(queries, "seq", axis=1, tiled=True)[0]
    total_rows = all_queries.shape[0]
    query_heads = all_queries.reshape(total_rows, HEADS, HEAD)
    key_heads = keys_local.reshape(-1, HEADS, HEAD)
    value_heads = values_local.reshape(-1, HEADS, HEAD)
    scores = (
        jnp.einsum("qhd,khd->hqk", query_heads, key_heads, preferred_element_type=jnp.float32)
        * scale
    )
    scores = jnp.where(live_local[None, None, :], scores, -1e30)
    local_top = jnp.max(scores, axis=2)
    global_top = lax.pmax(local_top, "seq")
    weights = jnp.where(live_local[None, None, :], jnp.exp(scores - global_top[:, :, None]), 0.0)
    totals = jnp.sum(weights, axis=2)
    summed = jnp.einsum(
        "hqk,khd->qhd",
        weights.astype(jnp.bfloat16),
        value_heads,
        preferred_element_type=jnp.float32,
    )
    own_sums, own_totals = (
        lax.psum_scatter(summed.reshape(total_rows, width), "seq", scatter_dimension=0, tiled=True),
        lax.psum_scatter(totals.T, "seq", scatter_dimension=0, tiled=True),
    )
    mixed = (
        (own_sums.reshape(own_rows, HEADS, HEAD) / own_totals[:, :, None])
        .reshape(own_rows, width)
        .astype(jnp.bfloat16)
    )
    projected = jnp.dot(mixed, attn_out_weight, preferred_element_type=jnp.float32)
    onehot = (
        timestep[:, None] == jnp.arange(gate_table.shape[0], dtype=jnp.int32)[None, :]
    ).astype(jnp.float32)
    gate = jnp.dot(onehot, gate_table, precision=lax.Precision.HIGHEST)
    stream_out = (stream[0].astype(jnp.float32) + gate * projected).astype(jnp.bfloat16)[None]
    grad_in, grad_weight = critic_pass(critic_in, critic_cot, critic_weight)
    return (stream_out, grad_in, grad_weight)


def step_kernel(
    zs,
    parts,
    stream_hbm,
    queries,
    new_keys,
    new_values,
    cache_keys,
    cache_values,
    frames_hbm,
    group_hbm,
    timestep_hbm,
    gate_hbm,
    out_weight_hbm,
    critic_in,
    critic_cot,
    weight_hbm,
    stream_out,
    grad_in,
    grad_weight,
    cot,
    wdiag,
    cin,
    out_weight,
    wfull,
    gmine,
    psend,
    precv,
    dsend,
    xsend,
    ysend,
    rdiag,
    rx,
    ry,
    osum,
    zsend,
    zrecv,
    q_all,
    q_other,
    kfull,
    vfull,
    frames,
    live_row,
    asend,
    arecv,
    mixed,
    stream,
    gate_table,
    group_index,
    timestep,
    send_sems,
    recv_sems,
    local_sems,
):
    f32, bf16 = jnp.float32, jnp.bfloat16
    dp, seq = lax.axis_index("dp"), lax.axis_index("seq")
    z, core = seq // 2, lax.rem(seq, 2)
    other = 1 - core
    tokens, width = cin.shape
    block = width // 4
    half = width // 2
    own_q = queries.shape[0]
    cached, fresh = cache_keys.shape[0], new_keys.shape[0]
    keys_one = cached + fresh
    heads_here = half // HEAD
    zh = zs // 2
    dp_x = dp + 1 - 2 * lax.rem(dp, 2)
    dp_y = lax.rem(dp + 2, 4)
    dp_d = dp_x + 2 - 4 * (dp_x // 2)
    order = (dp_d, dp_x, dp_y, dp)
    xn, yn, pair = (dp_x, seq), (dp_y, seq), (dp, z * 2 + other)

    near = z + 1 - 2 * lax.rem(z, 2)
    across = zs - 1 - z
    far = zs - 1 - near
    inner = (z == 1) | (z == 2)
    to_near, to_across = (dp, near * 2 + core), (dp, across * 2 + core)
    second = jnp.where(inner, across, far)
    third = jnp.where(inner, far, across)
    held = (z, near, second, third)

    other_cols = pl.ds(pl.multiple_of(other * half, 128), half)
    own_cols = pl.ds(pl.multiple_of(core * half, 128), half)

    started = []

    def load(src, dst):
        copy = pltpu.make_async_copy(src, dst, local_sems.at[len(started)])
        copy.start()
        started.append(copy)
        return copy

    def columns(b):
        return pl.ds(pl.multiple_of(order[b] * block, 128), block)

    weight_load = load(weight_hbm, wfull.at[dp, z, core])
    q_load = load(queries.at[:, own_cols], q_all.at[seq])
    q_other_load = load(queries.at[:, other_cols], q_other)
    cot_load = load(critic_cot, cot)
    cin_loads = [load(critic_in.at[:, columns(b)], cin.at[:, columns(b)]) for b in range(4)]
    small_loads = [
        load(cache_keys.at[:, own_cols], kfull.at[pl.ds(0, cached)]),
        load(new_keys.at[:, own_cols], kfull.at[pl.ds(cached, fresh)]),
        load(cache_values.at[:, own_cols], vfull.at[pl.ds(0, cached)]),
        load(new_values.at[:, own_cols], vfull.at[pl.ds(cached, fresh)]),
        load(frames_hbm, frames.at[0]),
        load(group_hbm, group_index),
        load(timestep_hbm, timestep),
        load(gate_hbm, gate_table),
        load(stream_hbm, stream),
        load(out_weight_hbm, out_weight),
    ]

    barrier = pltpu.get_barrier_semaphore()
    peers = [xn, yn, pair]
    for j in range(1, zs):
        zt = lax.rem(z + j, zs)
        peers += [(dp, zt * 2 + core), (dp, zt * 2 + other)]
    for peer in peers:
        pl.semaphore_signal(
            barrier, inc=1, device_id=peer, device_id_type=pl.DeviceIdType.MESH
        )
    pl.semaphore_wait(barrier, len(peers))

    sent = []

    def remote(src, dst, slot, peer, n):
        return pltpu.make_async_remote_copy(
            src_ref=src,
            dst_ref=dst,
            send_sem=send_sems.at[n],
            recv_sem=recv_sems.at[slot],
            device_id=peer,
            device_id_type=pl.DeviceIdType.MESH,
        )

    def send(src, dst, slot, peer, when=None):
        copy = remote(src, dst, slot, peer, len(sent))
        if when is None:
            copy.start()
        else:
            pl.when(when)(copy.start)
        sent.append((copy, when))

    def arrived(dst, slot):
        remote(dst, dst, slot, pair, 0).wait_recv()

    W_Z, W_X, W_Y, W_P = 0, zs, 2 * zs, 3 * zs
    W_PX, W_PY, W_D, W_PD = 4 * zs, 5 * zs, 6 * zs, 7 * zs
    Q_Z, KV_P = 8 * zs, 10 * zs
    G_P = 10 * zs + 5
    G_D, G_X, G_Y, G_Z = G_P + 4 * zs, G_P + 5 * zs, G_P + 6 * zs, G_P + 7 * zs
    A_Z = G_P + 8 * zs

    q_load.wait()
    q_other_load.wait()
    for chip, when in ((near, None), (across, inner)):
        send(q_all.at[seq], q_all.at[seq], Q_Z + seq, (dp, chip * 2 + core), when)
        send(q_other, q_all.at[seq], Q_Z + seq, (dp, chip * 2 + other), when)
    send(q_other, q_all.at[seq], Q_Z + seq, pair)
    mine = wfull.at[dp, z, core]
    weight_load.wait()
    send(mine, mine, W_Z + z, to_near)
    send(mine, mine, W_Z + z, to_across, inner)
    send(mine, mine, W_X, xn)
    send(mine, mine, W_Y, yn)
    send(mine, mine, W_P, pair)

    def grad_block(b):
        cin_loads[b].wait()
        acc = lax.dot_general(
            cin[:, columns(b)],
            cot[...],
            (((0,), (0,)), ((), ())),
            preferred_element_type=f32,
        )
        shard = block // (2 * zs)
        for k in range(zs):
            lo = acc[2 * k * shard : (2 * k + 1) * shard]
            hi = acc[(2 * k + 1) * shard : (2 * k + 2) * shard]
            gmine[b, k] = jnp.where(core == 0, lo, hi)
            psend[b, k] = jnp.where(core == 0, hi, lo).astype(bf16)
        for k in range(zs):
            send(psend.at[b, k], precv.at[b, k], G_P + b * zs + k, pair)

    def chip_sum(b, k):
        arrived(precv.at[b, k], G_P + b * zs + k)
        return gmine[b, k] + precv[b, k].astype(f32)

    cot_load.wait()
    grad_block(0)

    grad_block(1)
    for k in (0, 3, 1, 2):
        dsend[k] = chip_sum(0, k).astype(bf16)
        send(dsend.at[k], rdiag.at[k], G_D + k, xn if k < zh else yn)
    grad_block(2)

    def send_x(k):
        total = chip_sum(1, k)
        if k >= zh:
            arrived(rdiag.at[k], G_D + k)
            total = total + rdiag[k].astype(f32)
        xsend[k] = total.astype(bf16)
        send(xsend.at[k], rx.at[k], G_X + k, xn)

    def send_y(k):
        total = chip_sum(2, k)
        if k < zh:
            arrived(rdiag.at[k], G_D + k)
            total = total + rdiag[k].astype(f32)
        ysend[k] = total.astype(bf16)
        send(ysend.at[k], ry.at[k], G_Y + k, yn)

    def line(of):
        def take(source):
            for ref, slot in of(source):
                arrived(ref, slot)

        def pass_on(source, peer):
            for ref, slot in of(source):
                send(ref, ref, slot, peer, inner)

        def first():
            take(near)
            pass_on(near, to_across)

        def inner_second():
            pl.when(inner)(lambda: take(across))
            pass_on(across, to_near)

        def both_third():
            take(far)
            pass_on(far, to_near)

        def outer_last():
            pl.when(jnp.logical_not(inner))(lambda: take(across))

        return first, inner_second, both_third, outer_last

    w_line = line(lambda s: [(wfull.at[dp, s, core], W_Z + s)])
    q_line = line(lambda s: [(q_all.at[2 * s + c], Q_Z + 2 * s + c) for c in range(2)])

    q_line[0]()
    q_line[1]()
    send_x(0)
    send_y(3)
    w_line[0]()
    w_line[1]()
    grad_block(3)
    q_line[2]()
    send(cache_keys.at[:, other_cols], kfull.at[pl.ds(keys_one, cached)], KV_P, pair)
    send(new_keys.at[:, other_cols], kfull.at[pl.ds(keys_one + cached, fresh)], KV_P + 1, pair)
    send(cache_values.at[:, other_cols], vfull.at[pl.ds(keys_one, cached)], KV_P + 2, pair)
    send(new_values.at[:, other_cols], vfull.at[pl.ds(keys_one + cached, fresh)], KV_P + 3, pair)
    send(frames_hbm, frames.at[1], KV_P + 4, pair)

    def attention():
        arrived(kfull.at[pl.ds(keys_one, cached)], KV_P)
        arrived(kfull.at[pl.ds(keys_one + cached, fresh)], KV_P + 1)
        arrived(vfull.at[pl.ds(keys_one, cached)], KV_P + 2)
        arrived(vfull.at[pl.ds(keys_one + cached, fresh)], KV_P + 3)
        arrived(frames.at[1], KV_P + 4)
        for copy in small_loads:
            copy.wait()
        first_frame = FRAMES_GROUP * group_index[0]
        live_row[...] = jnp.ones_like(live_row)
        for at, which in ((0, 0), (keys_one, 1)):
            f = frames[which]
            ok = (f < first_frame) & (f >= first_frame - WINDOW_FRAMES)
            live_row[:, at : at + cached] = jnp.where(ok, 1.0, 0.0)
        live = live_row[...] > 0.5
        rows_q = 2 * zs * own_q
        lane = lax.broadcasted_iota(jnp.int32, (rows_q, 128), 1)
        stats = jnp.zeros((rows_q, 128), f32)
        for h in range(heads_here):
            cols = slice(h * HEAD, (h + 1) * HEAD)
            q_head = q_all[:, :, cols].reshape(rows_q, HEAD)
            scores = lax.dot_general(
                q_head, kfull[:, cols], (((1,), (1,)), ((), ())), preferred_element_type=f32
            ) * (HEAD ** (-0.5))
            scores = jnp.where(live, scores, -1e30)
            top = jnp.max(scores, axis=1, keepdims=True)
            weights = jnp.where(live, jnp.exp(scores - top), 0.0)
            total = jnp.sum(weights, axis=1, keepdims=True)
            summed = jnp.dot(weights.astype(bf16), vfull[:, cols], preferred_element_type=f32)
            asend[:, :, cols] = summed.astype(bf16).reshape(2 * zs, own_q, HEAD)
            for at, value in ((0, top), (64, total)):
                for part in range(3):
                    piece = value.astype(bf16).astype(f32)
                    stats = jnp.where(lane == at + 16 * part + h, piece, stats)
                    value = value - piece
        asend[:, :, half:] = stats.astype(bf16).reshape(2 * zs, own_q, 128)
        for zt in (near, second, third):
            for ct in (core, other):
                at = zt * 2 + ct
                send(asend.at[at], arecv.at[seq], A_Z + seq, (dp, at))
        send(asend.at[z * 2 + other], arecv.at[seq], A_Z + seq, pair)
        arecv[seq] = asend[seq]

    send_y(0)
    send_x(3)
    send_x(1)
    send_y(2)
    w_line[2]()
    arrived(q_all.at[z * 2 + other], Q_Z + z * 2 + other)
    q_line[3]()
    attention()
    send_y(1)
    send_x(2)

    def w_out(j):
        shard_ref = wfull.at[dp, held[j], core]
        send(shard_ref, shard_ref, W_X + j, xn)
        send(shard_ref, shard_ref, W_Y + j, yn)
        send(shard_ref, shard_ref, W_P + j, pair)

    w_out(1)
    w_line[3]()
    w_out(2)
    w_out(3)

    def grad_in_block(b):
        rows = wfull[order[b]].reshape(block, width)
        step = 512

        def body(t, carry):
            at = pl.ds(pl.multiple_of(t * step, step), step)
            grad_in[at, columns(b)] = lax.dot_general(
                cot[at], rows, (((1,), (1,)), ((), ())), preferred_element_type=f32
            ).astype(bf16)
            return carry

        lax.fori_loop(0, tokens // step, body, 0)

    for j in range(zs):
        arrived(wfull.at[dp, held[j], other], W_P + j)
    grad_in_block(3)

    for k in (0, 3, 1, 2):
        arrived(rx.at[k], G_X + k)
        arrived(ry.at[k], G_Y + k)
        osum[k] = chip_sum(3, k) + rx[k].astype(f32) + ry[k].astype(f32)

        @pl.when(z != k)
        def _():
            zsend[k] = osum[k].astype(bf16)

        send(zsend.at[k], zrecv.at[z], G_Z + z, (dp, 2 * k + core), z != k)

    def from_sides(j):
        arrived(wfull.at[dp_x, held[j], core], W_X + j)
        shard_ref = wfull.at[dp_x, held[j], core]
        if j < zh:
            send(shard_ref, wdiag.at[held[j], core], W_D + j, yn)
        send(shard_ref, shard_ref, W_PX + j, pair)
        arrived(wfull.at[dp_y, held[j], core], W_Y + j)
        shard_ref = wfull.at[dp_y, held[j], core]
        if j >= zh:
            send(shard_ref, wdiag.at[held[j], core], W_D + j, xn)
        send(shard_ref, shard_ref, W_PY + j, pair)

    def grad_in_sides():
        for j in range(zs):
            arrived(wfull.at[dp_x, held[j], other], W_PX + j)
            arrived(wfull.at[dp_y, held[j], other], W_PY + j)
        rows = jnp.concatenate(
            [wfull[dp_x].reshape(block, width), wfull[dp_y].reshape(block, width)]
        )
        step = 512

        def body(t, carry):
            at = pl.ds(pl.multiple_of(t * step, step), step)
            both = lax.dot_general(
                cot[at], rows, (((1,), (1,)), ((), ())), preferred_element_type=f32
            ).astype(bf16)
            grad_in[at, columns(1)] = both[:, :block]
            grad_in[at, columns(2)] = both[:, block:]
            return carry

        lax.fori_loop(0, tokens // step, body, 0)

    def attention_out():
        for zt in (near, second, third):
            for ct in (core, other):
                arrived(arecv.at[zt * 2 + ct], A_Z + zt * 2 + ct)
        arrived(arecv.at[z * 2 + other], A_Z + z * 2 + other)

        def stat(zt, ct, at, h):
            s = arecv[zt * 2 + ct, :, half:].astype(f32)
            return s[:, at + h : at + h + 1] + (
                s[:, at + 16 + h : at + 17 + h] + s[:, at + 32 + h : at + 33 + h]
            )

        for ct in range(2):
            for h in range(heads_here):
                cols = slice(h * HEAD, (h + 1) * HEAD)
                tops = [stat(zt, ct, 0, h) for zt in range(zs)]
                sums = [stat(zt, ct, 64, h) for zt in range(zs)]
                top = functools.reduce(jnp.maximum, tops)
                acc = jnp.zeros((own_q, HEAD), f32)
                total = jnp.zeros((own_q, 1), f32)
                for zt in range(zs):
                    scale = jnp.exp(tops[zt] - top)
                    acc = acc + scale * arecv[zt * 2 + ct, :, cols].astype(f32)
                    total = total + scale * sums[zt]
                mixed[:, ct * half + h * HEAD : ct * half + (h + 1) * HEAD] = (acc / total).astype(bf16)
        gate = jnp.zeros((1, width), f32)
        for s in range(gate_table.shape[0]):
            gate = gate + jnp.where(timestep[0] == s, gate_table[s : s + 1], 0.0)
        projected = jnp.dot(mixed[...], out_weight[...], preferred_element_type=f32)
        stream_out[...] = (stream[...].astype(f32) + gate * projected).astype(bf16)
    from_sides(0)
    from_sides(1)
    from_sides(2)
    attention_out()
    from_sides(3)

    grad_in_sides()
    for j in range(zs):
        shard_ref = wdiag.at[held[j], core]
        arrived(shard_ref, W_D + j)
        send(shard_ref, shard_ref, W_PD + j, pair)

    factor = float(tokens * parts) ** (-0.5)
    grad = osum[z]
    for zt in (near, second, third):
        arrived(zrecv.at[zt], G_Z + zt)
        grad = grad + zrecv[zt].astype(f32)
    grad_weight[...] = grad * factor

    for j in range(zs):
        arrived(wdiag.at[held[j], other], W_PD + j)

    for copy, when in sent:
        if when is None:
            copy.wait_send()
        else:
            pl.when(when)(copy.wait_send)


def finish_kernel(
    stream_part,
    grad_part,
    weight_part,
    cot,
    wdiag,
    stream_out,
    grad_in,
    grad_weight,
    last,
    sems,
):
    tokens, width = cot.shape
    block = width // 4
    dp = lax.axis_index("dp")
    dp_x = dp + 1 - 2 * lax.rem(dp, 2)
    dp_y = lax.rem(dp + 2, 4)
    dp_d = dp_x + 2 - 4 * (dp_x // 2)
    copies = []

    def put(src, dst):
        copy = pltpu.make_async_copy(src, dst, sems.at[len(copies)])
        copy.start()
        copies.append(copy)

    def columns(b):
        return pl.ds(pl.multiple_of(b * block, 128), block)

    for b in (dp, dp_x, dp_y):
        put(grad_part.at[:, columns(b)], grad_in.at[:, columns(b)])
    put(stream_part, stream_out)
    put(weight_part, grad_weight)
    rows = wdiag[...].reshape(block, width)
    pieces = 4
    step = tokens // pieces
    for t in range(pieces):
        at = slice(t * step, (t + 1) * step)
        last[at] = lax.dot_general(
            cot[at], rows, (((1,), (1,)), ((), ())), preferred_element_type=jnp.float32
        ).astype(last.dtype)
        put(last.at[at], grad_in.at[at, columns(dp_d)])
    for copy in copies:
        copy.wait()


def fused(
    stream,
    queries,
    new_keys,
    new_values,
    cache_keys,
    cache_values,
    cache_frames,
    group_index,
    timestep,
    gate_table,
    attn_out_weight,
    critic_in,
    critic_cot,
    critic_weight,
):
    bf16, f32 = jnp.bfloat16, jnp.float32
    zs = lax.axis_size("seq") // 2
    parts = lax.axis_size(("dp", "seq"))
    tokens, width = critic_in.shape
    own_q = queries.shape[1]
    shard = critic_weight.shape[0]
    cached, fresh = cache_keys.shape[1], new_keys.shape[1]
    half = width // 2
    keys_two = 2 * (cached + fresh)
    vmem, smem = pltpu.VMEM, pltpu.SMEM
    hbm = pl.BlockSpec(memory_space=pltpu.HBM)
    shards = (zs, shard, width)
    parts_out = pl.pallas_call(
        functools.partial(step_kernel, zs, parts),
        out_shape=(
            vmem((own_q, width), bf16),
            vmem((tokens, width), bf16),
            vmem((shard, width), f32),
            vmem((tokens, width), bf16),
            vmem((zs, 2, shard, width), bf16),
        ),
        in_specs=[hbm] * 14,
        out_specs=(pl.BlockSpec(memory_space=vmem),) * 5,
        scratch_shapes=[
            vmem((tokens, width), bf16),
            vmem((width, width), bf16),
            vmem((4, zs, 2, shard, width), bf16),
            vmem((4,) + shards, f32),
            vmem((4,) + shards, bf16),
            vmem((4,) + shards, bf16),
            vmem(shards, bf16),
            vmem(shards, bf16),
            vmem(shards, bf16),
            vmem(shards, bf16),
            vmem(shards, bf16),
            vmem(shards, bf16),
            vmem(shards, f32),
            vmem(shards, bf16),
            vmem(shards, bf16),
            vmem((2 * zs, own_q, half), bf16),
            vmem((own_q, half), bf16),
            vmem((keys_two, half), bf16),
            vmem((keys_two, half), bf16),
            vmem((2, 1, cached), jnp.int32),
            vmem((1, keys_two), f32),
            vmem((2 * zs, own_q, half + 128), bf16),
            vmem((2 * zs, own_q, half + 128), bf16),
            vmem((own_q, width), bf16),
            vmem((own_q, width), bf16),
            vmem(gate_table.shape, f32),
            smem((1,), jnp.int32),
            smem((1,), jnp.int32),
            pltpu.SemaphoreType.DMA((120,)),
            pltpu.SemaphoreType.DMA((20 * zs + 5,)),
            pltpu.SemaphoreType.DMA((18,)),
        ],
        compiler_params=pltpu.CompilerParams(
            collective_id=0, has_side_effects=True, vmem_limit_bytes=VMEM_LIMIT
        ),
    )(
        *(
            a if a.shape == (1,) else pltpu.with_memory_space_constraint(a, pltpu.HBM)
            for a in (
                stream[0],
                queries[0],
                new_keys[0],
                new_values[0],
                cache_keys[0],
                cache_values[0],
                cache_frames,
                group_index,
                timestep,
                gate_table,
                attn_out_weight,
                critic_in,
                critic_cot,
                critic_weight,
            )
        )
    )
    stream_out, grad_in, grad_weight = pl.pallas_call(
        finish_kernel,
        out_shape=(
            jax.ShapeDtypeStruct((own_q, width), bf16),
            jax.ShapeDtypeStruct((tokens, width), bf16),
            jax.ShapeDtypeStruct((shard, width), f32),
        ),
        in_specs=[pl.BlockSpec(memory_space=vmem)] * 5,
        out_specs=(hbm,) * 3,
        scratch_shapes=[
            vmem((tokens, width // 4), bf16),
            pltpu.SemaphoreType.DMA((9,)),
        ],
        compiler_params=pltpu.CompilerParams(vmem_limit_bytes=FINISH_LIMIT),
    )(*(pltpu.with_memory_space_constraint(a, vmem) for a in parts_out))
    return (stream_out[None], grad_in, grad_weight)


def local(*args):
    shard, tokens = args[13].shape[0], args[11].shape[0]
    fits = (
        lax.axis_size("dp") == 4
        and lax.axis_size("seq") == 8
        and shard % 16 == 0
        and args[1].shape[1] % 16 == 0
        and args[4].shape[1] % 16 == 0
        and args[1].shape[2] % 512 == 0
        and tokens % 256 == 0
    )
    return fused(*args) if fits else by_collectives(*args)


def solution(mesh):
    return jax.shard_map(
        local,
        mesh=mesh,
        in_specs=(
            P("dp", "seq", None),
            P("dp", "seq", None),
            P("dp", "seq", None),
            P("dp", "seq", None),
            P("dp", "seq", None),
            P("dp", "seq", None),
            P("dp", "seq"),
            P("dp"),
            P("dp"),
            P(),
            P(),
            P(("dp", "seq"), None),
            P(("dp", "seq"), None),
            P(("dp", "seq"), None),
        ),
        out_specs=(P("dp", "seq", None), P(("dp", "seq"), None), P(("dp", "seq"), None)),
        check_vma=False,
    )
```

time: 66.7 us -> 53.9 us (0.81)
  the two profiles are of different devices: /device:TPU:31 before, /device:TPU:0 now
where the time goes in v1:
time: 53.9 us; the launch traced here: 53.7 us
  Pallas kernels  51.8 us (96%)
  between operations  1.93 us (4%)
    pallas_call x1, Pallas kernels, fused(): pl.pallas_call(functools.partial(step_kernel, zs, parts), out_shape=(vmem...  49.2 us
    pallas_call x1, Pallas kernels, fused(): pl.pallas_call(finish_kernel, out_shape=(jax.ShapeDtypeStruct((own_q, wid...  2.55 us

profile of v1, /device:TPU:0, one launch (start us, length us, event | category | flops | bytes accessed | tf_op | source)
XLA Modules:
  0.0 53.7 jit_solution(14039869017616662500)
XLA Ops:
  1.9 49.2 %shard_map.157 = (bf16[32,1536]{1,0:T(8,128)(2,1)S(1)}, bf16[1024,1536]{1,0:T(8,128)(2,1)S(1)}, f32[48,1536]{1,0:T(8,128)S(1)}, bf16[1024,1536]{1,0:T(8,128)(2,1)S(1)}, bf16[4,2,48,1536]{3,2,1,0:T(8,128)(2,1)S(1)}) custom-call(bf16[32,1536]{1,0:T(8,128)(2,1)} %bitcast.9, bf16[32,1536]{1,0:T(8,128)(2,1)} %bitcast.10, bf16[32,1536]{1,0:T(8,128)(2,1)} %bitcast.11, ...), custom_call_target="tpu_custom_call" | custom-call | tf_op jit(solution)/shard_map/pallas_call | solution.py:615
  51.2 2.6 %shard_map.158 = (bf16[32,1536]{1,0:T(8,128)(2,1)}, bf16[1024,1536]{1,0:T(8,128)(2,1)}, f32[48,1536]{1,0:T(8,128)}) custom-call(bf16[32,1536]{1,0:T(8,128)(2,1)S(1)} %get-tuple-element.11.stream_part, bf16[1024,1536]{1,0:T(8,128)(2,1)S(1)} %get-tuple-element.12.grad_part, f32[48,1536]{1,0:T(8,128)S(1)} %get-tuple-element.13.weight_part, ...), custom_call_target="tpu_custom_call" | custom-call | tf_op jit(solution)/shard_map/pallas_call | solution.py:683

commit v2 on v1

--- a/solution.py
+++ b/solution.py
@@ -12,6 +12,7 @@
 FRAMES_GROUP = 3
 WINDOW_FRAMES = 9
 VMEM_LIMIT = 44 * 1024 * 1024
+EARLY = 128
 FINISH_LIMIT = 8 * 1024 * 1024
 
 
@@ -135,6 +136,7 @@
     osum,
     zsend,
     zrecv,
+    chain,
     q_all,
     q_other,
     kfull,
@@ -159,6 +161,8 @@
     tokens, width = cin.shape
     block = width // 4
     half = width // 2
+    whole, early = pl.ds(0, width), pl.ds(width - EARLY, EARLY)
+    late = pl.ds(0, width - EARLY)
     own_q = queries.shape[0]
     cached, fresh = cache_keys.shape[0], new_keys.shape[0]
     keys_one = cached + fresh
@@ -174,6 +178,7 @@
     across = zs - 1 - z
     far = zs - 1 - near
     inner = (z == 1) | (z == 2)
+    outer = jnp.logical_not(inner)
     to_near, to_across = (dp, near * 2 + core), (dp, across * 2 + core)
     second = jnp.where(inner, across, far)
     third = jnp.where(inner, far, across)
@@ -222,7 +227,7 @@
         )
     pl.semaphore_wait(barrier, len(peers))
 
-    sent = []
+    groups = {}
 
     def remote(src, dst, slot, peer, n):
         return pltpu.make_async_remote_copy(
@@ -234,37 +239,72 @@
             device_id_type=pl.DeviceIdType.MESH,
         )
 
-    def send(src, dst, slot, peer, when=None):
-        copy = remote(src, dst, slot, peer, len(sent))
+    def send(src, dst, slot, peer, group, when=None):
+        n = groups.setdefault(group, len(groups))
+        copy = remote(src, dst, slot, peer, n)
         if when is None:
             copy.start()
         else:
             pl.when(when)(copy.start)
-        sent.append((copy, when))
+
+    def all_sent():
+        eight = precv.at[pl.ds(0, 2)]
+        twelve = precv.at[pl.ds(0, 3)]
+        three = pl.ds(0, 3)
+        totals = {
+            "own": (eight, None),
+            "one": (precv.at[0, 0], None),
+            "line": (precv.at[0], inner),
+            "psend": (precv, None),
+            "sums": (twelve, None),
+            "late": (precv.at[:, :, :, late], None),
+            "diag": (precv.at[0, :, :, late], None),
+            "chip1": (precv.at[0, 0], z != 1),
+            "chip2": (precv.at[0, 0], z != 2),
+            "start": (precv.at[0, 0], outer),
+            "far": (precv.at[0, 0], inner),
+            "near": (precv.at[0, 0], inner),
+            "early": (precv.at[three, :, :, early], None),
+            "early0": (precv.at[0, 0, :, early], None),
+            "earlyd": (precv.at[0, 0, :, early], None),
+            "fline": (precv.at[three, :, :, early], inner),
+            "q": (q_all.at[three], None),
+            "qline": (q_all, inner),
+            "k": (kfull.at[pl.ds(0, keys_one)], None),
+            "v": (vfull.at[pl.ds(0, keys_one)], None),
+            "frames": (frames.at[0], None),
+            "parts": (arecv.at[pl.ds(0, 2 * zs - 1)], None),
+        }
+        for group, n in groups.items():
+            view, when = totals[group]
+            wait = remote(view, view, 0, pair, n).wait_send
+            if when is None:
+                wait()
+            else:
+                pl.when(when)(wait)
 
     def arrived(dst, slot):
         remote(dst, dst, slot, pair, 0).wait_recv()
 
-    W_Z, W_X, W_Y, W_P = 0, zs, 2 * zs, 3 * zs
-    W_PX, W_PY, W_D, W_PD = 4 * zs, 5 * zs, 6 * zs, 7 * zs
-    Q_Z, KV_P = 8 * zs, 10 * zs
-    G_P = 10 * zs + 5
-    G_D, G_X, G_Y, G_Z = G_P + 4 * zs, G_P + 5 * zs, G_P + 6 * zs, G_P + 7 * zs
-    A_Z = G_P + 8 * zs
+    W_Z, W_X, W_Y, F_Z, Q_Z = 0, zs, 2 * zs, 3 * zs, 4 * zs
+    G_P, G_D, G_X, G_Y = 6 * zs, 10 * zs, 11 * zs, 12 * zs
+    W_P, W_PX, W_PY, W_PD, W_D, F_OWN = (13 * zs + i for i in range(6))
+    K_P, V_P, FRAMES_P, A_Z, G_Z = (13 * zs + 6 + i for i in range(5))
+    C_FAR, C_MID, C_END = (13 * zs + 11 + i for i in range(3))
 
     q_load.wait()
     q_other_load.wait()
     for chip, when in ((near, None), (across, inner)):
-        send(q_all.at[seq], q_all.at[seq], Q_Z + seq, (dp, chip * 2 + core), when)
-        send(q_other, q_all.at[seq], Q_Z + seq, (dp, chip * 2 + other), when)
-    send(q_other, q_all.at[seq], Q_Z + seq, pair)
+        send(q_all.at[seq], q_all.at[seq], Q_Z + seq, (dp, chip * 2 + core), "qline" if when is not None else "q", when)
+        send(q_other, q_all.at[seq], Q_Z + seq, (dp, chip * 2 + other), "qline" if when is not None else "q", when)
+    send(q_other, q_all.at[seq], Q_Z + seq, pair, "q")
     mine = wfull.at[dp, z, core]
     weight_load.wait()
-    send(mine, mine, W_Z + z, to_near)
-    send(mine, mine, W_Z + z, to_across, inner)
-    send(mine, mine, W_X, xn)
-    send(mine, mine, W_Y, yn)
-    send(mine, mine, W_P, pair)
+    send(mine, mine, W_Z + z, to_near, "own")
+    send(mine, mine, W_Z + z, to_across, "line", inner)
+    send(mine, mine, W_X, xn, "own")
+    send(mine, mine, W_Y, yn, "own")
+    send(mine, mine, W_P, pair, "own")
 
     def grad_block(b):
         cin_loads[b].wait()
@@ -281,7 +321,7 @@
             gmine[b, k] = jnp.where(core == 0, lo, hi)
             psend[b, k] = jnp.where(core == 0, hi, lo).astype(bf16)
         for k in range(zs):
-            send(psend.at[b, k], precv.at[b, k], G_P + b * zs + k, pair)
+            send(psend.at[b, k], precv.at[b, k], G_P + b * zs + k, pair, "psend")
 
     def chip_sum(b, k):
         arrived(precv.at[b, k], G_P + b * zs + k)
@@ -289,12 +329,6 @@
 
     cot_load.wait()
     grad_block(0)
-
-    grad_block(1)
-    for k in (0, 3, 1, 2):
-        dsend[k] = chip_sum(0, k).astype(bf16)
-        send(dsend.at[k], rdiag.at[k], G_D + k, xn if k < zh else yn)
-    grad_block(2)
 
     def send_x(k):
         total = chip_sum(1, k)
@@ -302,7 +336,7 @@
             arrived(rdiag.at[k], G_D + k)
             total = total + rdiag[k].astype(f32)
         xsend[k] = total.astype(bf16)
-        send(xsend.at[k], rx.at[k], G_X + k, xn)
+        send(xsend.at[k], rx.at[k], G_X + k, xn, "sums")
 
     def send_y(k):
         total = chip_sum(2, k)
@@ -310,16 +344,19 @@
             arrived(rdiag.at[k], G_D + k)
             total = total + rdiag[k].astype(f32)
         ysend[k] = total.astype(bf16)
-        send(ysend.at[k], ry.at[k], G_Y + k, yn)
-
-    def line(of):
+        send(ysend.at[k], ry.at[k], G_Y + k, yn, "sums")
+
+    def line(of, group):
         def take(source):
+            if group == "fline":
+                arrived(precv.at[0, pl.ds(0, 3), :, early], F_Z + source)
+                return
             for ref, slot in of(source):
                 arrived(ref, slot)
 
         def pass_on(source, peer):
             for ref, slot in of(source):
-                send(ref, ref, slot, peer, inner)
+                send(ref, ref, slot, peer, group, inner)
 
         def first():
             take(near)
@@ -334,13 +371,59 @@
             pass_on(far, to_near)
 
         def outer_last():
-            pl.when(jnp.logical_not(inner))(lambda: take(across))
-
-        return first, inner_second, both_third, outer_last
-
-    w_line = line(lambda s: [(wfull.at[dp, s, core], W_Z + s)])
-    q_line = line(lambda s: [(q_all.at[2 * s + c], Q_Z + 2 * s + c) for c in range(2)])
-
+            pl.when(outer)(lambda: take(across))
+
+        def inner_third():
+            pl.when(inner)(lambda: take(far))
+            pass_on(far, to_near)
+
+        def outer_third():
+            pl.when(outer)(lambda: take(far))
+
+        return first, inner_second, both_third, outer_last, inner_third, outer_third
+
+    def early_pieces(s, c):
+        return [
+            (wfull.at[dp_x, s, c, :, early], F_Z + s),
+            (wfull.at[dp_y, s, c, :, early], F_Z + s),
+            (wdiag.at[s, c, :, early], F_Z + s),
+        ]
+
+    def early_diag():
+        arrived(wfull.at[dp_x, z, core], W_X)
+        arrived(wfull.at[dp_y, z, core], W_Y)
+        for way, peer, when in ((dp_x, yn, core == 0), (dp_y, xn, core == 1)):
+            send(
+                wfull.at[way, z, core, :, early], wdiag.at[z, core, :, early], F_OWN, peer, "earlyd", when
+            )
+
+    def early_own():
+        arrived(wdiag.at[z, core, :, early], F_OWN)
+        for ref, slot in early_pieces(z, core):
+            send(ref, ref, slot, to_near, "early")
+            send(ref, ref, slot, to_across, "fline", inner)
+
+    def early_to_pair(j):
+        pieces = early_pieces(held[j], core)
+        for (ref, _), slot in zip(pieces, (W_PX, W_PY, W_PD)):
+            if j or slot == W_PD:
+                send(ref, ref, slot, pair, "early" if j else "early0")
+
+    f_line = line(lambda s: early_pieces(s, core), "fline")
+    w_line = line(lambda s: [(wfull.at[dp, s, core], W_Z + s)], "line")
+    q_line = line(lambda s: [(q_all.at[2 * s + c], Q_Z + 2 * s + c) for c in range(2)], "qline")
+
+    def send_diag(k):
+        dsend[k] = chip_sum(0, k).astype(bf16)
+        send(dsend.at[k], rdiag.at[k], G_D + k, xn if k < zh else yn, "sums")
+
+    grad_block(1)
+    send_diag(0)
+    send_diag(3)
+    grad_block(2)
+    early_diag()
+    send_diag(1)
+    send_diag(2)
     q_line[0]()
     q_line[1]()
     send_x(0)
@@ -349,18 +432,17 @@
     w_line[1]()
     grad_block(3)
     q_line[2]()
-    send(cache_keys.at[:, other_cols], kfull.at[pl.ds(keys_one, cached)], KV_P, pair)
-    send(new_keys.at[:, other_cols], kfull.at[pl.ds(keys_one + cached, fresh)], KV_P + 1, pair)
-    send(cache_values.at[:, other_cols], vfull.at[pl.ds(keys_one, cached)], KV_P + 2, pair)
-    send(new_values.at[:, other_cols], vfull.at[pl.ds(keys_one + cached, fresh)], KV_P + 3, pair)
-    send(frames_hbm, frames.at[1], KV_P + 4, pair)
+    early_own()
+    send(cache_keys.at[:, other_cols], kfull.at[pl.ds(keys_one, cached)], K_P, pair, "k")
+    send(new_keys.at[:, other_cols], kfull.at[pl.ds(keys_one + cached, fresh)], K_P, pair, "k")
+    send(cache_values.at[:, other_cols], vfull.at[pl.ds(keys_one, cached)], V_P, pair, "v")
+    send(new_values.at[:, other_cols], vfull.at[pl.ds(keys_one + cached, fresh)], V_P, pair, "v")
+    send(frames_hbm, frames.at[1], FRAMES_P, pair, "frames")
 
     def attention():
-        arrived(kfull.at[pl.ds(keys_one, cached)], KV_P)
-        arrived(kfull.at[pl.ds(keys_one + cached, fresh)], KV_P + 1)
-        arrived(vfull.at[pl.ds(keys_one, cached)], KV_P + 2)
-        arrived(vfull.at[pl.ds(keys_one + cached, fresh)], KV_P + 3)
-        arrived(frames.at[1], KV_P + 4)
+        arrived(kfull.at[pl.ds(keys_one, keys_one)], K_P)
+        arrived(vfull.at[pl.ds(keys_one, keys_one)], V_P)
+        arrived(frames.at[1], FRAMES_P)
         for copy in small_loads:
             copy.wait()
         first_frame = FRAMES_GROUP * group_index[0]
@@ -394,8 +476,8 @@
         for zt in (near, second, third):
             for ct in (core, other):
                 at = zt * 2 + ct
-                send(asend.at[at], arecv.at[seq], A_Z + seq, (dp, at))
-        send(asend.at[z * 2 + other], arecv.at[seq], A_Z + seq, pair)
+                send(asend.at[at], arecv.at[seq], A_Z, (dp, at), "parts")
+        send(asend.at[z * 2 + other], arecv.at[seq], A_Z, pair, "parts")
         arecv[seq] = asend[seq]
 
     send_y(0)
@@ -405,21 +487,23 @@
     w_line[2]()
     arrived(q_all.at[z * 2 + other], Q_Z + z * 2 + other)
     q_line[3]()
+    f_line[0]()
+    f_line[1]()
     attention()
     send_y(1)
     send_x(2)
 
     def w_out(j):
+        piece = wfull.at[dp, held[j], core, :, late]
+        send(piece, piece, W_X + j, xn, "late")
+        send(piece, piece, W_Y + j, yn, "late")
         shard_ref = wfull.at[dp, held[j], core]
-        send(shard_ref, shard_ref, W_X + j, xn)
-        send(shard_ref, shard_ref, W_Y + j, yn)
-        send(shard_ref, shard_ref, W_P + j, pair)
+        send(shard_ref, shard_ref, W_P, pair, "own")
 
     w_out(1)
     w_line[3]()
     w_out(2)
     w_out(3)
-
     def grad_in_block(b):
         rows = wfull[order[b]].reshape(block, width)
         step = 512
@@ -433,37 +517,64 @@
 
         lax.fori_loop(0, tokens // step, body, 0)
 
-    for j in range(zs):
-        arrived(wfull.at[dp, held[j], other], W_P + j)
+    arrived(wfull.at[dp, :, other], W_P)
     grad_in_block(3)
 
-    for k in (0, 3, 1, 2):
+    def own_sum(k):
         arrived(rx.at[k], G_X + k)
         arrived(ry.at[k], G_Y + k)
         osum[k] = chip_sum(3, k) + rx[k].astype(f32) + ry[k].astype(f32)
 
+    def to_chip(k):
+        own_sum(k)
+
         @pl.when(z != k)
         def _():
             zsend[k] = osum[k].astype(bf16)
 
-        send(zsend.at[k], zrecv.at[z], G_Z + z, (dp, 2 * k + core), z != k)
+        send(zsend.at[k], zrecv.at[z], G_Z, (dp, 2 * k + core), "chip%d" % k, z != k)
+
+    def chain_start():
+        @pl.when(outer)
+        def _():
+            zsend[0] = osum[across].astype(bf16)
+
+        send(zsend.at[0], chain.at[0], C_FAR, to_near, "start", outer)
+
+    def chain_far():
+        @pl.when(inner)
+        def _():
+            arrived(chain.at[0], C_FAR)
+            zsend[0] = (osum[far] + chain[0].astype(f32)).astype(bf16)
+
+        send(zsend.at[0], chain.at[1], C_MID, to_across, "far", inner)
+
+    def chain_near():
+        @pl.when(inner)
+        def _():
+            arrived(chain.at[1], C_MID)
+            zsend[zs - 1] = (osum[near] + chain[1].astype(f32)).astype(bf16)
+
+        send(zsend.at[zs - 1], chain.at[2], C_END, to_near, "near", inner)
 
     def from_sides(j):
-        arrived(wfull.at[dp_x, held[j], core], W_X + j)
-        shard_ref = wfull.at[dp_x, held[j], core]
+        cols = late if j else whole
+        piece = wfull.at[dp_x, held[j], core, :, cols]
+        arrived(piece, W_X + j) if j else None
         if j < zh:
-            send(shard_ref, wdiag.at[held[j], core], W_D + j, yn)
-        send(shard_ref, shard_ref, W_PX + j, pair)
-        arrived(wfull.at[dp_y, held[j], core], W_Y + j)
-        shard_ref = wfull.at[dp_y, held[j], core]
+            on = wfull.at[dp_x, held[j], core, :, late]
+            send(on, wdiag.at[held[j], core, :, late], W_D, yn, "late")
+        send(piece, piece, W_PX, pair, "late" if j else "own")
+        piece = wfull.at[dp_y, held[j], core, :, cols]
+        arrived(piece, W_Y + j) if j else None
         if j >= zh:
-            send(shard_ref, wdiag.at[held[j], core], W_D + j, xn)
-        send(shard_ref, shard_ref, W_PY + j, pair)
+            on = wfull.at[dp_y, held[j], core, :, late]
+            send(on, wdiag.at[held[j], core, :, late], W_D, xn, "late")
+        send(piece, piece, W_PY, pair, "late" if j else "one")
 
     def grad_in_sides():
-        for j in range(zs):
-            arrived(wfull.at[dp_x, held[j], other], W_PX + j)
-            arrived(wfull.at[dp_y, held[j], other], W_PY + j)
+        arrived(wfull.at[dp_x, :, other], W_PX)
+        arrived(wfull.at[dp_y, :, other], W_PY)
         rows = jnp.concatenate(
             [wfull[dp_x].reshape(block, width), wfull[dp_y].reshape(block, width)]
         )
@@ -481,10 +592,7 @@
         lax.fori_loop(0, tokens // step, body, 0)
 
     def attention_out():
-        for zt in (near, second, third):
-            for ct in (core, other):
-                arrived(arecv.at[zt * 2 + ct], A_Z + zt * 2 + ct)
-        arrived(arecv.at[z * 2 + other], A_Z + z * 2 + other)
+        arrived(arecv.at[pl.ds(0, 2 * zs - 1)], A_Z)
 
         def stat(zt, ct, at, h):
             s = arecv[zt * 2 + ct, :, half:].astype(f32)
@@ -510,33 +618,48 @@
             gate = gate + jnp.where(timestep[0] == s, gate_table[s : s + 1], 0.0)
         projected = jnp.dot(mixed[...], out_weight[...], preferred_element_type=f32)
         stream_out[...] = (stream[...].astype(f32) + gate * projected).astype(bf16)
+    def finish_grad():
+        factor = float(tokens * parts) ** (-0.5)
+
+        @pl.when(inner)
+        def _():
+            grad = osum[z]
+            arrived(zrecv.at[pl.ds(0, zs - 1)], G_Z)
+            for zt in (near, second, third):
+                grad = grad + zrecv[zt].astype(f32)
+            grad_weight[...] = grad * factor
+
+        @pl.when(outer)
+        def _():
+            arrived(chain.at[2], C_END)
+            grad_weight[...] = (osum[z] + chain[2].astype(f32)) * factor
+
+    own_sum(0)
+    own_sum(3)
+    chain_start()
+    f_line[4]()
     from_sides(0)
+    to_chip(1)
+    to_chip(2)
     from_sides(1)
+    chain_far()
     from_sides(2)
     attention_out()
     from_sides(3)
-
+    chain_near()
+    f_line[5]()
+    f_line[3]()
+    for j in range(zs):
+        early_to_pair(j)
     grad_in_sides()
+    arrived(wdiag.at[:, core, :, late], W_D)
     for j in range(zs):
-        shard_ref = wdiag.at[held[j], core]
-        arrived(shard_ref, W_D + j)
-        send(shard_ref, shard_ref, W_PD + j, pair)
-
-    factor = float(tokens * parts) ** (-0.5)
-    grad = osum[z]
-    for zt in (near, second, third):
-        arrived(zrecv.at[zt], G_Z + zt)
-        grad = grad + zrecv[zt].astype(f32)
-    grad_weight[...] = grad * factor
-
-    for j in range(zs):
-        arrived(wdiag.at[held[j], other], W_PD + j)
-
-    for copy, when in sent:
-        if when is None:
-            copy.wait_send()
-        else:
-            pl.when(when)(copy.wait_send)
+        ref = wdiag.at[held[j], core, :, late]
+        send(ref, ref, W_PD, pair, "diag")
+    finish_grad()
+    arrived(wdiag.at[:, other], W_PD)
+
+    all_sent()
 
 
 def finish_kernel(
@@ -639,6 +762,7 @@
             vmem(shards, f32),
             vmem(shards, bf16),
             vmem(shards, bf16),
+            vmem((3, shard, width), bf16),
             vmem((2 * zs, own_q, half), bf16),
             vmem((own_q, half), bf16),
             vmem((keys_two, half), bf16),
@@ -652,8 +776,8 @@
             vmem(gate_table.shape, f32),
             smem((1,), jnp.int32),
             smem((1,), jnp.int32),
-            pltpu.SemaphoreType.DMA((120,)),
-            pltpu.SemaphoreType.DMA((20 * zs + 5,)),
+            pltpu.SemaphoreType.DMA((22,)),
+            pltpu.SemaphoreType.DMA((13 * zs + 14,)),
             pltpu.SemaphoreType.DMA((18,)),
         ],
         compiler_params=pltpu.CompilerParams(

time: 53.9 us -> 51.8 us (0.961)
  Pallas kernels: 51.8 us -> 49.7 us
    pallas_call x1, Pallas kernels: 49.2 us -> 47.1 us  [fused(): pl.pallas_call(functools.partial(step_kernel, zs, parts), out_shape=(vmem...]
where the time goes in v2:
time: 51.8 us; the launch traced here: 51.6 us
  Pallas kernels  49.7 us (96%)
  between operations  1.93 us (4%)
    pallas_call x1, Pallas kernels, fused(): pl.pallas_call(functools.partial(step_kernel, zs, parts), out_shape=(vmem...  47.1 us
    pallas_call x1, Pallas kernels, fused(): pl.pallas_call(finish_kernel, out_shape=(jax.ShapeDtypeStruct((own_q, wid...  2.55 us

profile of v2, /device:TPU:0, one launch (start us, length us, event | category | flops | bytes accessed | tf_op | source)
XLA Modules:
  0.0 51.6 jit_solution(14898904946874764872)
XLA Ops:
  1.9 47.1 %shard_map.157 = (bf16[32,1536]{1,0:T(8,128)(2,1)S(1)}, bf16[1024,1536]{1,0:T(8,128)(2,1)S(1)}, f32[48,1536]{1,0:T(8,128)S(1)}, bf16[1024,1536]{1,0:T(8,128)(2,1)S(1)}, bf16[4,2,48,1536]{3,2,1,0:T(8,128)(2,1)S(1)}) custom-call(bf16[32,1536]{1,0:T(8,128)(2,1)} %bitcast.9, bf16[32,1536]{1,0:T(8,128)(2,1)} %bitcast.10, bf16[32,1536]{1,0:T(8,128)(2,1)} %bitcast.11, ...), custom_call_target="tpu_custom_call" | custom-call | tf_op jit(solution)/shard_map/pallas_call | solution.py:738
  49.1 2.6 %shard_map.158 = (bf16[32,1536]{1,0:T(8,128)(2,1)}, bf16[1024,1536]{1,0:T(8,128)(2,1)}, f32[48,1536]{1,0:T(8,128)}) custom-call(bf16[32,1536]{1,0:T(8,128)(2,1)S(1)} %get-tuple-element.11.stream_part, bf16[1024,1536]{1,0:T(8,128)(2,1)S(1)} %get-tuple-element.12.grad_part, f32[48,1536]{1,0:T(8,128)S(1)} %get-tuple-element.13.weight_part, ...), custom_call_target="tpu_custom_call" | custom-call | tf_op jit(solution)/shard_map/pallas_call | solution.py:807

commit v3 on v2

--- a/solution.py
+++ b/solution.py
@@ -12,7 +12,7 @@
 FRAMES_GROUP = 3
 WINDOW_FRAMES = 9
 VMEM_LIMIT = 44 * 1024 * 1024
-EARLY = 128
+EARLY = 256
 FINISH_LIMIT = 8 * 1024 * 1024
 
 
@@ -217,15 +217,21 @@
     ]
 
     barrier = pltpu.get_barrier_semaphore()
-    peers = [xn, yn, pair]
-    for j in range(1, zs):
-        zt = lax.rem(z + j, zs)
-        peers += [(dp, zt * 2 + core), (dp, zt * 2 + other)]
-    for peer in peers:
+    def greet(peer):
         pl.semaphore_signal(
             barrier, inc=1, device_id=peer, device_id_type=pl.DeviceIdType.MESH
         )
-    pl.semaphore_wait(barrier, len(peers))
+
+    peers = [xn, yn, pair, to_near, (dp, near * 2 + other)]
+    for peer in peers:
+        greet(peer)
+
+    @pl.when(inner)
+    def _():
+        greet(to_across)
+        greet((dp, across * 2 + other))
+
+    pl.semaphore_wait(barrier, len(peers) + 2 * inner.astype(jnp.int32))
 
     groups = {}
 

time: 51.8 us -> 51.4 us (level)
  no operation moved by 1% of the time
where the time goes in v3:
time: 51.4 us; the launch traced here: 51.3 us
  Pallas kernels  49.3 us (96%)
  between operations  1.93 us (4%)
    pallas_call x1, Pallas kernels, fused(): pl.pallas_call(functools.partial(step_kernel, zs, parts), out_shape=(vmem...  46.8 us
    pallas_call x1, Pallas kernels, fused(): pl.pallas_call(finish_kernel, out_shape=(jax.ShapeDtypeStruct((own_q, wid...  2.55 us

profile of v3, /device:TPU:0, one launch (start us, length us, event | category | flops | bytes accessed | tf_op | source)
XLA Modules:
  0.0 51.3 jit_solution(4718546972645179443)
XLA Ops:
  1.9 46.8 %shard_map.157 = (bf16[32,1536]{1,0:T(8,128)(2,1)S(1)}, bf16[1024,1536]{1,0:T(8,128)(2,1)S(1)}, f32[48,1536]{1,0:T(8,128)S(1)}, bf16[1024,1536]{1,0:T(8,128)(2,1)S(1)}, bf16[4,2,48,1536]{3,2,1,0:T(8,128)(2,1)S(1)}) custom-call(bf16[32,1536]{1,0:T(8,128)(2,1)} %bitcast.9, bf16[32,1536]{1,0:T(8,128)(2,1)} %bitcast.10, bf16[32,1536]{1,0:T(8,128)(2,1)} %bitcast.11, ...), custom_call_target="tpu_custom_call" | custom-call | tf_op jit(solution)/shard_map/pallas_call | solution.py:744
  48.7 2.6 %shard_map.158 = (bf16[32,1536]{1,0:T(8,128)(2,1)}, bf16[1024,1536]{1,0:T(8,128)(2,1)}, f32[48,1536]{1,0:T(8,128)}) custom-call(bf16[32,1536]{1,0:T(8,128)(2,1)S(1)} %get-tuple-element.11.stream_part, bf16[1024,1536]{1,0:T(8,128)(2,1)S(1)} %get-tuple-element.12.grad_part, f32[48,1536]{1,0:T(8,128)S(1)} %get-tuple-element.13.weight_part, ...), custom_call_target="tpu_custom_call" | custom-call | tf_op jit(solution)/shard_map/pallas_call | solution.py:813
